TPU v7x, 8 devices: a whole 2x2x1 slice. The times are simulated.
8 devices in a mesh: dp: 1 (over z), ep: 8 (over y, x, core).
Axes of the slice: x: 2, y: 2, z: 1, core: 2. Of those that a mesh axis runs over, the one named last changes fastest.
Arguments:
- tokens: bfloat16 [8, 512, 2048], P(('dp', 'ep'))
- w_query: bfloat16 [2048, 16, 256], P('ep')
- w_key: bfloat16 [2048, 16, 256], P('ep')
- w_value: bfloat16 [2048, 16, 256], P('ep')
- w_out: bfloat16 [4096, 2048], P('ep')
- w_router: float32 [2048, 512], replicated
- w_one: bfloat16 [512, 2048, 128], P('ep')
- w_three: bfloat16 [512, 2048, 128], P('ep')
- w_two: bfloat16 [512, 128, 2048], P('ep')
- expert_ids: int32 [8, 512, 10], P(('dp', 'ep'))
Outputs:
- output: bfloat16 [8, 512, 2048], P(('dp', 'ep'))
All inputs are finite; a program needn't handle non-finite values.
Results may differ from a plain program's by a relative error of at most 0.00951267.
Values are sent between devices in bfloat16 or wider.
A program may use at most 1 GiB of HBM per device.

v0:
```python
import jax
import jax.numpy as jnp
from jax import lax
from jax.sharding import PartitionSpec as P

EPS = 1e-6


def rms_norm(vals):
    wide = vals.astype(jnp.float32)
    return wide * lax.rsqrt(jnp.mean(wide * wide, axis=-1, keepdims=True) + EPS)


def attention_layer(tokens, w_query, w_key, w_value, w_out):
    seq_count = tokens.shape[0]
    seq_len = tokens.shape[1]
    head_dim = w_query.shape[2]
    normed = rms_norm(tokens).astype(jnp.bfloat16)
    query = jnp.einsum('bsd,dhk->bshk', normed, w_query, preferred_element_type=jnp.float32).astype(jnp.bfloat16)
    keys = jnp.einsum('bsd,dhk->bshk', normed, w_key, preferred_element_type=jnp.float32).astype(jnp.bfloat16)
    values = jnp.einsum('bsd,dhk->bshk', normed, w_value, preferred_element_type=jnp.float32).astype(jnp.bfloat16)
    scores = jnp.einsum('bqhk,bshk->bhqs', query, keys, preferred_element_type=jnp.float32) * head_dim ** -0.5
    causal = lax.broadcasted_iota(jnp.int32, (seq_len, seq_len), 0) >= lax.broadcasted_iota(jnp.int32, (seq_len, seq_len), 1)
    attn_weights = jax.nn.softmax(jnp.where(causal, scores, -jnp.inf), axis=-1).astype(jnp.bfloat16)
    context = jnp.einsum('bhqs,bshk->bqhk', attn_weights, values, preferred_element_type=jnp.float32).astype(jnp.bfloat16)
    attn_out = jnp.einsum('crd,de->cre', context.reshape(seq_count, seq_len, -1), w_out, preferred_element_type=jnp.float32)
    return (tokens.astype(jnp.float32) + attn_out).astype(jnp.bfloat16)


def router_gates(hidden, w_router, expert_ids):
    normed = rms_norm(hidden)
    logits = jnp.einsum('bsd,de->bse', normed, w_router, precision=lax.Precision.HIGHEST, preferred_element_type=jnp.float32)
    chosen = jnp.take_along_axis(logits, expert_ids, axis=-1)
    return normed.astype(jnp.bfloat16), jax.nn.softmax(chosen, axis=-1)


def dispatch_tables(ids_flat, experts, cap_rows):
    member = jnp.sum((ids_flat[:, :, None] == jnp.arange(experts, dtype=jnp.int32)).astype(jnp.int32), axis=1)
    before = jnp.cumsum(member, axis=0) - member
    slot = jnp.take_along_axis(before, ids_flat, axis=1)
    onehot = (member[:, :, None] > 0) & (before[:, :, None] == jnp.arange(cap_rows, dtype=jnp.int32))
    return onehot.astype(jnp.bfloat16), ids_flat * cap_rows + slot


def expert_ffn(rows, w_one, w_three, w_two):
    first = jnp.einsum('end,edf->enf', rows, w_one, preferred_element_type=jnp.float32)
    third = jnp.einsum('end,edf->enf', rows, w_three, preferred_element_type=jnp.float32)
    activated = (jax.nn.silu(first) * third).astype(jnp.bfloat16)
    return jnp.einsum('enf,efd->end', activated, w_two, preferred_element_type=jnp.float32).astype(jnp.bfloat16)


def combine_rows(hidden_flat, back_rows, flat_slot, gates_flat):
    table = back_rows.reshape(-1, back_rows.shape[-1])
    picked = jnp.take(table, flat_slot, axis=0)
    mixed = jnp.sum(gates_flat[:, :, None] * picked.astype(jnp.float32), axis=1)
    return (hidden_flat.astype(jnp.float32) + mixed).astype(jnp.bfloat16)


def solution(mesh):
    tok_spec = P(('dp', 'ep'))
    row_spec = P('ep')

    def local_layer(tokens, w_query, w_key, w_value, w_out, w_router, w_one, w_three, w_two, expert_ids):
        full_query = lax.all_gather(w_query, 'ep', axis=0, tiled=True)
        full_key = lax.all_gather(w_key, 'ep', axis=0, tiled=True)
        full_value = lax.all_gather(w_value, 'ep', axis=0, tiled=True)
        full_out = lax.all_gather(w_out, 'ep', axis=0, tiled=True)
        hidden = attention_layer(tokens, full_query, full_key, full_value, full_out)
        normed, gates = router_gates(hidden, w_router, expert_ids)
        seq_count, seq_len, model_dim = tokens.shape
        choices = expert_ids.shape[2]
        experts = w_router.shape[1]
        tok_count = seq_count * seq_len
        cap_rows = 2 * tok_count * choices // experts
        onehot, flat_slot = dispatch_tables(expert_ids.reshape(tok_count, choices), experts, cap_rows)
        send_rows = jnp.einsum('tec,td->ecd', onehot, normed.reshape(tok_count, model_dim), preferred_element_type=jnp.float32).astype(jnp.bfloat16)
        recv_rows = lax.all_to_all(send_rows, 'ep', 0, 1, tiled=True)
        done_rows = expert_ffn(recv_rows, w_one, w_three, w_two)
        back_rows = lax.all_to_all(done_rows, 'ep', 1, 0, tiled=True)
        layer_out = combine_rows(hidden.reshape(tok_count, model_dim), back_rows, flat_slot, gates.reshape(tok_count, choices))
        return layer_out.reshape(seq_count, seq_len, model_dim)

    return jax.shard_map(local_layer, mesh=mesh, in_specs=(tok_spec, row_spec, row_spec, row_spec, row_spec, P(), row_spec, row_spec, row_spec, tok_spec), out_specs=tok_spec, check_vma=False)
```

profile of v0, /device:TPU:0, one launch (start us, length us, event | category | flops | bytes accessed | tf_op | source)
XLA Modules:
  0.0 2010.6 jit_solution(17700619989394905720)
XLA Ops:
  6.5 0.7 all-gather.9.cloned.1.call-update
  7.3 0.7 all-gather.7.cloned.1.call-update
  8.1 0.7 all-gather.5.cloned.1.call-update
  8.8 0.5 all-gather.11.cloned.1.call-update
  9.3 1.6 convert_reduce_fusion
  10.9 0.3 copy.113
  11.4 0.4 copy.117
  11.8 0.7 fusion.46
  12.7 0.3 copy.111
  13.0 0.3 copy.112
  13.4 0.8 iota_compare_fusion.2
  14.1 2.1 fusion.24
  16.2 0.2 bitcast_subtract_fusion
  16.5 79.6 %all-gather.9.cloned.1.call-done = bf16[2048,16,256]{2,1,0:T(8,128)(2,1)} async-done(((bf16[256,16,256]{2,1,0:T(8,128)(2,1)}), bf16[2048,16,256]{2,1,0:T(8,128)(2,1)}) %all-gather.9.cloned.1.call-update) | async-done | bytes 16777232 | tf_op jit(solution)/shard_map/all_gather | solution.py:65
  96.1 14.6 fusion.7
  110.7 71.3 %all-gather.7.cloned.1.call-done = bf16[2048,16,256]{2,1,0:T(8,128)(2,1)} async-done(((bf16[256,16,256]{2,1,0:T(8,128)(2,1)}), bf16[2048,16,256]{2,1,0:T(8,128)(2,1)}) %all-gather.7.cloned.1.call-update) | async-done | bytes 16777232 | tf_op jit(solution)/shard_map/all_gather | solution.py:64
  182.0 19.2 fusion.29
  201.2 18.0 fusion.70
  219.2 48.7 %all-gather.5.cloned.1.call-done = bf16[2048,16,256]{2,1,0:T(8,128)(2,1)} async-done(((bf16[256,16,256]{2,1,0:T(8,128)(2,1)}), bf16[2048,16,256]{2,1,0:T(8,128)(2,1)}) %all-gather.5.cloned.1.call-update) | async-done | bytes 16777232 | tf_op jit(solution)/shard_map/all_gather | solution.py:66
  267.9 20.7 %fusion.37 = bf16[16,256,512]{2,1,0:T(8,128)(2,1)} fusion(f32[16,512,512]{1,2,0:T(8,128)} %get-tuple-element.10, f32[16,512]{1,0:T(8,128)S(1)} %get-tuple-element.9, bf16[2048,16,256]{2,1,0:T(8,128)(2,1)} %all-gather.5.cloned.1.call-done, bf16[1,512,2048]{2,1,0:T(8,128)(2,1)S(1)} %copy-done.2, f32[512]{0:T(512)S(1)} %add_rsqrt_fusion.1), kind=kOutput, calls=%fused_computation.50 | convolution fusion | flops 10753146880 | bytes 39880704 | tf_op jit(solution)/shard_map/bhqs,bshk->bqhk/dot_general | solution.py:25
  288.7 65.1 %all-gather.11.cloned.1.call-done = bf16[4096,2048]{1,0:T(8,128)(2,1)} async-done(((bf16[512,2048]{1,0:T(8,128)(2,1)}), bf16[4096,2048]{1,0:T(8,128)(2,1)}) %all-gather.11.cloned.1.call-update) | async-done | bytes 16777232 | tf_op jit(solution)/shard_map/all_gather | solution.py:67
  353.7 14.9 fusion.27
  368.6 28.5 %convolution_convert_fusion = bf16[512,20,2048]{2,0,1:T(8,128)(2,1)} fusion(s32[512,512]{0,1:T(8,128)S(1)} %bitcast_subtract_fusion, pred[512,512]{0,1:T(8,128)(4,1)S(1)} %copy.117, bf16[1,512,2048]{2,1,0:T(8,128)(2,1)} %get-tuple-element.12, f32[512]{0:T(512)S(1)} %add_rsqrt_fusion), kind=kOutput, calls=%fused_computation.9 | convolution fusion | flops 21509439488 | bytes 45352960 | tf_op jit(solution)/shard_map/tec,td->ecd/dot_general | solution.py:76
  397.1 65.1 %copy.118 = bf16[512,20,2048]{2,1,0:T(8,128)(2,1)} copy(bf16[512,20,2048]{2,0,1:T(8,128)(2,1)} %convolution_convert_fusion) | data formatting | bytes 83886080 | tf_op jit(solution)/shard_map/convert_element_type | solution.py:76
  462.2 556.5 %all_to_all.33 = bf16[512,20,2048]{2,1,0:T(8,128)(2,1)} all-to-all(bf16[512,20,2048]{2,1,0:T(8,128)(2,1)} %copy.118), channel_id=1, replica_groups=mesh['dp'=1,'ep'=8] {'ep'}, dimensions={0} | all-to-all | bytes 83886080 | tf_op jit(solution)/shard_map/all_to_all | solution.py:77
  1018.8 41.1 %copy.120 = bf16[64,8,20,2048]{3,0,2,1:T(8,128)(2,1)} copy(bf16[64,8,20,2048]{3,2,0,1:T(8,128)(2,1)} %bitcast.80) | data formatting | bytes 83886080 | tf_op jit(solution)/shard_map/all_to_all | solution.py:77
  1059.9 70.0 %fusion.1 = f32[64,160,128]{2,1,0:T(8,128)} fusion(bf16[64,2048,128]{2,1,0:T(8,128)(2,1)} %param.17, bf16[64,160,2048]{2,0,1:T(8,128)(2,1)} %bitcast.81), kind=kOutput, calls=%fused_computation.5 | convolution fusion | flops 5368709120 | bytes 80740352 | tf_op jit(solution)/shard_map/end,edf->enf/dot_general | solution.py:47
  1129.9 79.9 %convolution_convert_fusion.1 = bf16[64,160,2048]{2,1,0:T(8,128)(2,1)} fusion(bf16[64,128,2048]{2,1,0:T(8,128)(2,1)} %param.18, f32[64,160,128]{2,1,0:T(8,128)} %fusion.1, bf16[64,2048,128]{2,1,0:T(8,128)(2,1)} %param.16, bf16[64,160,2048]{2,0,1:T(8,128)(2,1)} %bitcast.82), kind=kOutput, calls=%fused_computation.10 | convolution fusion | flops 10766254080 | bytes 156237824 | tf_op jit(solution)/shard_map/enf,efd->end/dot_general | solution.py:49
  1209.8 36.7 %copy.123 = bf16[64,160,2048]{2,0,1:T(8,128)(2,1)} copy(bf16[64,160,2048]{2,1,0:T(8,128)(2,1)} %convolution_convert_fusion.1) | data formatting | bytes 83886080 | tf_op jit(solution)/shard_map/convert_element_type | solution.py:49
  1246.5 7.0 all-to-all-start.1
  1253.7 0.2 reshape.270
  1253.9 41.2 %gather_fusion.2 = s32[5120]{0:T(1024)S(1)} fusion(s32[512,512]{0,1:T(8,128)S(1)} %copy-done.1, s32[5120]{0:T(1024)S(1)} %reshape.270), kind=kCustom, calls=%fused_computation.2 | custom fusion | bytes 81920 | tf_op jit(solution)/shard_map/jit(take_along_axis)/gather | solution.py:40
  1295.1 0.2 gather.16
  1295.3 0.2 reshape.273
  1295.7 0.2 reshape.264
  1296.2 0.2 reshape.256
  1296.5 0.8 copy.116
  1297.3 9.2 fusion.22
  1306.5 40.8 %gather_fusion.1 = f32[5120]{0:T(1024)S(1)} fusion(f32[512,512]{1,0:T(8,128)S(1)} %fusion.22, s32[5120]{0:T(1024)S(1)} %reshape.264), kind=kCustom, calls=%fused_computation.1 | custom fusion | bytes 81920 | tf_op jit(solution)/shard_map/jit(take_along_axis)/gather | solution.py:33
  1347.4 0.2 reshape.263
  1347.9 0.9 copy.129
  1348.7 358.6 %all-to-all-done.1 = bf16[64,160,2048]{2,0,1:T(8,128)(2,1)} async-done(((bf16[64,160,2048]{2,0,1:T(8,128)(2,1)}), bf16[64,160,2048]{2,0,1:T(8,128)(2,1)}, u32[]{:S(2)}, u32[]{:S(2)}) %all-to-all-start.1) | async-done | bytes 41943072 | tf_op jit(solution)/shard_map/all_to_all | solution.py:79
  1707.3 43.7 %copy.124 = bf16[8,64,20,2048]{3,2,1,0:T(8,128)(2,1)} copy(bf16[8,64,20,2048]{3,1,2,0:T(8,128)(2,1)} %bitcast.22) | data formatting | bytes 83886080 | tf_op jit(solution)/shard_map/all_to_all | solution.py:79
  1751.1 61.5 %reshape.253 = bf16[10240,2048]{1,0:T(8,128)(2,1)} reshape(bf16[8,64,20,2048]{3,2,1,0:T(8,128)(2,1)} %copy.124) | data formatting | bytes 83886080 | tf_op jit(solution)/shard_map/reshape | solution.py:53
  1812.6 119.6 %gather_fusion = bf16[5120,2048]{1,0:T(8,128)(2,1)} fusion(bf16[10240,2048]{1,0:T(8,128)(2,1)} %reshape.253, s32[5120]{0:T(1024)S(1)} %broadcast_clamp_fusion), kind=kCustom, calls=%fused_computation | custom fusion | bytes 41963520 | tf_op jit(solution)/shard_map/jit(_take)/gather | solution.py:54
  1932.2 34.1 %reshape.255 = bf16[512,10,2048]{2,1,0:T(8,128)(2,1)} reshape(bf16[5120,2048]{1,0:T(8,128)(2,1)} %gather_fusion) | data formatting | bytes 41943040 | tf_op jit(solution)/shard_map/jit(_take)/gather | solution.py:54
  1966.3 33.3 %multiply_reduce_fusion = f32[512,2048]{1,0:T(8,128)} fusion(bf16[512,10,2048]{2,1,0:T(8,128)(2,1)} %reshape.255, f32[512,10]{1,0:T(8,128)S(1)} %bitcast.87, pred[512,10]{1,0:T(8,128)(4,1)S(1)} %copy-done.8), kind=kLoop, calls=%fused_computation.4 | loop fusion | flops 40894464 | bytes 25191424 | tf_op jit(solution)/shard_map/reduce_sum | solution.py:55
  1999.6 4.2 fusion.28
  (48 shorter events, 1.6 us)
Async XLA Ops:
  6.5 2.8 copy-start.6
  6.5 89.6 %all-gather.9.cloned.1.call-start = ((), (), s32[]{:S(2)}) async-start(), calls=%async_computation.4 | async-start | bytes 18874368 | tf_op jit(solution)/shard_map/all_gather | solution.py:65
  7.3 174.8 %all-gather.7.cloned.1.call-start = ((), (), s32[]{:S(2)}) async-start(), calls=%async_computation.3 | async-start | bytes 18874368 | tf_op jit(solution)/shard_map/all_gather | solution.py:64
  8.0 259.9 %all-gather.5.cloned.1.call-start = ((), (), s32[]{:S(2)}) async-start(), calls=%async_computation.2 | async-start | bytes 18874368 | tf_op jit(solution)/shard_map/all_gather | solution.py:66
  8.7 345.0 %all-gather.11.cloned.1.call-start = ((), (), s32[]{:S(2)}) async-start(), calls=%async_computation.5 | async-start | bytes 18874368 | tf_op jit(solution)/shard_map/all_gather | solution.py:67
  16.4 352.2 %copy-start = (s32[512,512]{0,1:T(8,128)}, s32[512,512]{0,1:T(8,128)S(1)}, u32[]{:S(2)}) copy-start(s32[512,512]{0,1:T(8,128)S(1)} %bitcast_subtract_fusion) | copy-start | bytes 3145732
  16.4 165.6 %copy-start.2 = (bf16[1,512,2048]{2,1,0:T(8,128)(2,1)S(1)}, bf16[1,512,2048]{2,1,0:T(8,128)(2,1)}, u32[]{:S(2)}) copy-start(bf16[1,512,2048]{2,1,0:T(8,128)(2,1)} %param.10) | copy-start | bytes 6291460
  368.6 28.5 %copy-start.9 = (f32[512]{0:T(512)}, f32[512]{0:T(512)S(1)}, u32[]{:S(2)}) copy-start(f32[512]{0:T(512)S(1)} %add_rsqrt_fusion) | copy-start | bytes 6148
  1246.5 7.0 copy-start.7
  1246.5 7.4 copy-start.1
  1246.5 460.9 %all-to-all-start.1 = ((bf16[64,160,2048]{2,0,1:T(8,128)(2,1)}), bf16[64,160,2048]{2,0,1:T(8,128)(2,1)}, u32[]{:S(2)}, u32[]{:S(2)}) async-start(bf16[64,160,2048]{2,0,1:T(8,128)(2,1)} %copy.123), calls=%async_computation.1 | async-start | bytes 83886080 | tf_op jit(solution)/shard_map/all_to_all | solution.py:79
  1253.9 43.4 %copy-start.3 = (bf16[1,512,2048]{2,1,0:T(8,128)(2,1)S(1)}, bf16[1,512,2048]{2,1,0:T(8,128)(2,1)}, u32[]{:S(2)}) copy-start(bf16[1,512,2048]{2,1,0:T(8,128)(2,1)} %get-tuple-element.12) | copy-start | bytes 6291460
  1253.9 43.4 %copy-start.10 = (f32[512]{0:T(512)S(1)}, f32[512]{0:T(512)}, u32[]{:S(2)}) copy-start(f32[512]{0:T(512)} %copy-done.9) | copy-start | bytes 6148
  1932.2 34.1 %copy-start.5 = (f32[1,512,10]{2,1,0:T(8,128)S(1)}, f32[1,512,10]{2,1,0:T(8,128)}, u32[]{:S(2)}) copy-start(f32[1,512,10]{2,1,0:T(8,128)} %copy.129) | copy-start | bytes 61444
  1932.2 34.1 %copy-start.8 = (pred[512,10]{1,0:T(8,128)(4,1)S(1)}, pred[512,10]{1,0:T(8,128)(4,1)}, u32[]{:S(2)}) copy-start(pred[512,10]{1,0:T(8,128)(4,1)} %copy.116) | copy-start | bytes 15364
  1966.3 33.3 %copy-start.4 = (bf16[1,512,2048]{2,1,0:T(8,128)(2,1)S(1)}, bf16[1,512,2048]{2,1,0:T(8,128)(2,1)}, u32[]{:S(2)}) copy-start(bf16[1,512,2048]{2,1,0:T(8,128)(2,1)} %get-tuple-element.12) | copy-start | bytes 6291460
Sparse Core Ops, SparseCore 0:
  9.2 86.8 all-gather.8
  97.9 84.0 all-gather.6
  183.8 84.0 all-gather.4
  269.6 84.0 all-gather.10
where the time goes:
time: 2020 us; the launch traced here: 2010 us
  waiting for transfers between devices  626 us (31%)
  blocking collectives  557 us (28%)
  local copies, waits for them, and re-layouts  489 us (24%)
  matrix products  257 us (13%)
  other arithmetic  61.5 us (3%)
    all_to_all x1, blocking collectives, local_layer(): recv_rows = lax.all_to_all(send_rows, 'ep', 0, 1, tiled=True)  557 us
    all_to_all x1, waiting for transfers between devices, local_layer(): back_rows = lax.all_to_all(done_rows, 'ep', 1, 0, tiled=True)  359 us
    gather x2, local copies, waits for them, and re-layouts, combine_rows(): picked = jnp.take(table, flat_slot, axis=0)  154 us
    dot_general x1, matrix products, expert_ffn(): jnp.einsum('enf,efd->end', activated, w_two, preferred_element_type=jnp.f...  79.9 us
    all_gather x1, waiting for transfers between devices, local_layer(): full_key = lax.all_gather(w_key, 'ep', axis=0, tiled=True)  79.6 us
    all_gather x1, waiting for transfers between devices, local_layer(): full_query = lax.all_gather(w_query, 'ep', axis=0, tiled=True)  71.3 us
    dot_general x1, matrix products, expert_ffn(): jnp.einsum('end,edf->enf', rows, w_three, preferred_element_type=jnp.floa...  70 us
    convert_element_type x1, local copies, waits for them, and re-layouts, local_layer(): jnp.einsum('tec,td->ecd', onehot, normed.reshape(tok_count, model_dim), p...  65.1 us
  transfers between devices with their start and end apart: 5, of which 5 were waited for; matrix products, arithmetic and copies ran while one was open for 9% of the time, Pallas kernels for 0%

commit v1 on v0

v1 whole, which is shorter than its diff:
```python
import functools

import jax
import jax.numpy as jnp
from jax import lax
from jax.experimental import pallas as pl
from jax.experimental.pallas import tpu as pltpu
from jax.sharding import PartitionSpec as P

EPS = 1e-6
CAP = 20
LANES = 128
BATCH = 8


def rms_norm(vals):
    wide = vals.astype(jnp.float32)
    return wide * lax.rsqrt(jnp.mean(wide * wide, axis=-1, keepdims=True) + EPS)


def attention_layer(tokens, w_query, w_key, w_value, w_out):
    seq_count = tokens.shape[0]
    seq_len = tokens.shape[1]
    head_dim = w_query.shape[2]
    normed = rms_norm(tokens).astype(jnp.bfloat16)
    query = jnp.einsum('bsd,dhk->bshk', normed, w_query, preferred_element_type=jnp.float32).astype(jnp.bfloat16)
    keys = jnp.einsum('bsd,dhk->bshk', normed, w_key, preferred_element_type=jnp.float32).astype(jnp.bfloat16)
    values = jnp.einsum('bsd,dhk->bshk', normed, w_value, preferred_element_type=jnp.float32).astype(jnp.bfloat16)
    scores = jnp.einsum('bqhk,bshk->bhqs', query, keys, preferred_element_type=jnp.float32) * head_dim ** -0.5
    causal = lax.broadcasted_iota(jnp.int32, (seq_len, seq_len), 0) >= lax.broadcasted_iota(jnp.int32, (seq_len, seq_len), 1)
    attn_weights = jax.nn.softmax(jnp.where(causal, scores, -jnp.inf), axis=-1).astype(jnp.bfloat16)
    context = jnp.einsum('bhqs,bshk->bqhk', attn_weights, values, preferred_element_type=jnp.float32).astype(jnp.bfloat16)
    attn_out = jnp.einsum('crd,de->cre', context.reshape(seq_count, seq_len, -1), w_out, preferred_element_type=jnp.float32)
    return (tokens.astype(jnp.float32) + attn_out).astype(jnp.bfloat16)


def router_gates(hidden, w_router, expert_ids):
    normed = rms_norm(hidden)
    logits = jnp.dot(normed, w_router, precision=lax.Precision.HIGHEST, preferred_element_type=jnp.float32)
    picks = []
    lane = lax.broadcasted_iota(jnp.int32, logits.shape, 1)
    for j in range(expert_ids.shape[1]):
        picks.append(jnp.sum(jnp.where(lane == expert_ids[:, j:j + 1], logits, 0.0), axis=1))
    chosen = jnp.stack(picks, axis=1)
    return normed.astype(jnp.bfloat16), jax.nn.softmax(chosen, axis=-1)


def routing_tables(ids_all, base, local_experts, group):
    total, choices = ids_all.shape
    per_dev = total // group
    loc = (ids_all - base).reshape(group, per_dev, choices)
    eq = loc[:, :, :, None] == jnp.arange(local_experts, dtype=jnp.int32)
    tok = lax.broadcasted_iota(jnp.int32, (group, per_dev, choices), 0) * per_dev + lax.broadcasted_iota(jnp.int32, (group, per_dev, choices), 1)
    pack = lax.broadcasted_iota(jnp.int32, (group, per_dev, choices), 2) * (2 * total) + tok
    code = jnp.sum(jnp.where(eq, pack[:, :, :, None], 0), axis=2)
    member = jnp.sum(eq.astype(jnp.int32), axis=2)
    tri = (lax.broadcasted_iota(jnp.int32, (per_dev, per_dev), 0) > lax.broadcasted_iota(jnp.int32, (per_dev, per_dev), 1)).astype(jnp.bfloat16)
    before = jnp.einsum('uv,sve->sue', tri, member.astype(jnp.bfloat16), preferred_element_type=jnp.float32).astype(jnp.int32)
    place = jnp.where(member > 0, before, -1)
    slot = jnp.arange(CAP, dtype=jnp.int32)
    short = jnp.sum(jnp.where(place[:, :, None, :] == slot[None, None, :, None], code[:, :, None, :], 0), axis=1)
    counts = jnp.sum(member, axis=1)
    offs = jnp.cumsum(counts, axis=0) - counts
    dest = jnp.where(slot[None, :, None] < counts[:, None, :], offs[:, None, :] + slot[None, :, None], -1)
    cap_all = group * CAP
    dest = dest.reshape(group * CAP, local_experts)
    short = short.reshape(group * CAP, local_experts)
    hit = dest[:, :, None] == jnp.arange(cap_all, dtype=jnp.int32)
    table = jnp.sum(jnp.where(hit, short[:, :, None] + 1, 0), axis=0) - 1
    table = jnp.where(table < 0, total, table)
    return table, jnp.sum(counts, axis=0)


def moe_kernel(sizes, codes, counts, gates, u_hbm, w1_ref, w3_ref, w2_ref, out_hbm, u_ref, acc, xrow, xmat, orow, sem):
    total, cap_all, sub = sizes
    e = pl.program_id(0)
    mask = 2 * total - 1
    shift = (2 * total).bit_length() - 1

    @pl.when(e == 0)
    def _():
        load = pltpu.make_async_copy(u_hbm, u_ref.at[pl.ds(0, total)], sem)
        load.start()
        u_ref[pl.ds(total, 1)] = jnp.zeros((1,) + u_ref.shape[1:], u_ref.dtype)

        def clear(i, _):
            acc[pl.ds(i * 8, 8)] = jnp.zeros((8,) + acc.shape[1:], acc.dtype)
            return 0

        lax.fori_loop(0, total // 8, clear, 0)
        load.wait()

    rows = counts[e]
    blocks = (rows + (BATCH - 1)) // BATCH

    def gather(b, _):
        first = pl.multiple_of(b * BATCH, BATCH)
        for k in range(BATCH):
            t = codes[e * cap_all + first + k] & mask
            xrow[pl.ds(pl.multiple_of((first + k) * sub, sub), sub), :] = u_ref[t].astype(jnp.float32)
        return 0

    lax.fori_loop(0, blocks, gather, 0)

    def ffn(m):
        for c in range(sub):
            xmat[pl.ds(0, m), c * LANES:(c + 1) * LANES] = xrow[pl.ds(c, m, stride=sub), :].astype(jnp.bfloat16)
        w13 = jnp.concatenate([w1_ref[0], w3_ref[0]], axis=1)
        both = jnp.dot(xmat[pl.ds(0, m), :], w13, preferred_element_type=jnp.float32)
        first, third = both[:, :LANES], both[:, LANES:]
        act = (first * jax.nn.sigmoid(first) * third).astype(jnp.bfloat16)
        done = jnp.dot(act, w2_ref[0], preferred_element_type=jnp.float32)
        for c in range(sub):
            part = done[:, c * LANES:(c + 1) * LANES].astype(jnp.bfloat16).astype(jnp.float32)
            orow[pl.ds(c, m, stride=sub), :] = part

    steps = (48, 96, cap_all)
    low = 0
    for m in steps:
        @pl.when((rows > low) & (rows <= m))
        def _(m=m):
            ffn(m)
        low = m

    def scatter(b, _):
        first = pl.multiple_of(b * BATCH, BATCH)
        toks, vals = [], []
        for k in range(BATCH):
            code = codes[e * cap_all + first + k]
            t = code & mask
            g = gates[(code >> shift) * total + t]
            toks.append(t)
            vals.append(acc[t] + g * orow[pl.ds(pl.multiple_of((first + k) * sub, sub), sub), :])
        for k in range(BATCH):
            acc[toks[k]] = vals[k]
        return 0

    lax.fori_loop(0, blocks, scatter, 0)

    @pl.when(e == pl.num_programs(0) - 1)
    def _():
        store = pltpu.make_async_copy(acc.at[pl.ds(0, total)], out_hbm, sem)
        store.start()
        store.wait()


def moe_partial(u_rows, gates_flat, codes, counts, w_one, w_three, w_two):
    total, sub, _ = u_rows.shape
    local, model_dim, ff = w_one.shape
    cap_all = codes.shape[0] // local
    return pl.pallas_call(
        functools.partial(moe_kernel, (total, cap_all, sub)),
        out_shape=jax.ShapeDtypeStruct((total, sub, LANES), jnp.float32),
        grid=(local,),
        in_specs=[
            pl.BlockSpec(memory_space=pltpu.SMEM),
            pl.BlockSpec(memory_space=pltpu.SMEM),
            pl.BlockSpec(memory_space=pltpu.SMEM),
            pl.BlockSpec(memory_space=pl.ANY),
            pl.BlockSpec((1, model_dim, ff), lambda e: (e, 0, 0)),
            pl.BlockSpec((1, model_dim, ff), lambda e: (e, 0, 0)),
            pl.BlockSpec((1, ff, model_dim), lambda e: (e, 0, 0)),
        ],
        out_specs=pl.BlockSpec(memory_space=pl.ANY),
        scratch_shapes=[
            pltpu.VMEM((total + 8, sub, LANES), jnp.bfloat16),
            pltpu.VMEM((total + 8, sub, LANES), jnp.float32),
            pltpu.VMEM((cap_all * sub, LANES), jnp.float32),
            pltpu.VMEM((cap_all, model_dim), jnp.bfloat16),
            pltpu.VMEM((cap_all * sub, LANES), jnp.float32),
            pltpu.SemaphoreType.DMA,
        ],
        compiler_params=pltpu.CompilerParams(dimension_semantics=('arbitrary',), vmem_limit_bytes=67043328),
        cost_estimate=pl.CostEstimate(flops=6 * 96 * local * model_dim * ff, bytes_accessed=150_000_000, transcendentals=0),
        name='moe_partial',
    )(codes, counts, gates_flat, u_rows, w_one, w_three, w_two)


def solution(mesh):
    tok_spec = P(('dp', 'ep'))
    row_spec = P('ep')
    group = mesh.shape['ep']

    def local_layer(tokens, w_query, w_key, w_value, w_out, w_router, w_one, w_three, w_two, expert_ids):
        seq_count, seq_len, model_dim = tokens.shape
        choices = expert_ids.shape[2]
        tok_count = seq_count * seq_len
        local = w_one.shape[0]
        ids = expert_ids.reshape(tok_count, choices)
        ids_all = lax.all_gather(ids, 'ep', axis=0, tiled=True)
        codes, counts = routing_tables(ids_all, lax.axis_index('ep') * local, local, group)
        full_query = lax.all_gather(w_query, 'ep', axis=0, tiled=True)
        full_key = lax.all_gather(w_key, 'ep', axis=0, tiled=True)
        full_value = lax.all_gather(w_value, 'ep', axis=0, tiled=True)
        full_out = lax.all_gather(w_out, 'ep', axis=0, tiled=True)
        hidden = attention_layer(tokens, full_query, full_key, full_value, full_out).reshape(tok_count, model_dim)
        normed, gates = router_gates(hidden, w_router, ids)
        u_rows = lax.all_gather(normed.reshape(tok_count, model_dim // LANES, LANES), 'ep', axis=0, tiled=True)
        gates_all = lax.all_gather(gates.T, 'ep', axis=1, tiled=True)
        partial = moe_partial(u_rows, gates_all.reshape(-1), codes.reshape(-1), counts, w_one, w_three, w_two)
        mixed = lax.psum_scatter(partial, 'ep', scatter_dimension=0, tiled=True)
        layer_out = (hidden.astype(jnp.float32) + mixed.reshape(tok_count, model_dim)).astype(jnp.bfloat16)
        return layer_out.reshape(seq_count, seq_len, model_dim)

    return jax.shard_map(local_layer, mesh=mesh, in_specs=(tok_spec, row_spec, row_spec, row_spec, row_spec, P(), row_spec, row_spec, row_spec, tok_spec), out_specs=tok_spec, check_vma=False)
```

time: 2020 us -> 806 us (0.40)
  blocking collectives: 557 us -> 25.8 us
  local copies, waits for them, and re-layouts: 489 us -> 7.1 us
  matrix products: 257 us -> 81.4 us
  Pallas kernels: 0 us -> 118 us
  waiting for transfers between devices: 626 us -> 510 us
  other arithmetic: 61.5 us -> 40.4 us
    all_to_all x1 -> x0, blocking collectives: 557 us -> none  [local_layer(): recv_rows = lax.all_to_all(send_rows, 'ep', 0, 1, tiled=True)]
    all_to_all x1 -> x0, waiting for transfers between devices: 359 us -> none  [local_layer(): back_rows = lax.all_to_all(done_rows, 'ep', 1, 0, tiled=True)]
    gather x14 -> x0, local copies, waits for them, and re-layouts: 237 us -> none  [the longest x2 154 us: combine_rows(): picked = jnp.take(table, flat_slot, axis=0)]
    reduce_scatter x0 -> x1, waiting for transfers between devices: none -> 204 us  [local_layer(): mixed = lax.psum_scatter(partial, 'ep', scatter_dimension=0, tiled=True)]
    dot_general x4 -> x2, matrix products: 188 us -> 13.8 us  [the longest x1 11.8 us: router_gates(): jnp.dot(normed, w_router, precision=lax.Precision.HIGHEST, preferred_elem...]
    pallas_call x0 -> x1, Pallas kernels: none -> 118 us  [moe_partial(): pl.pallas_call(functools.partial(moe_kernel, (total, cap_all, sub)), out_...]
    convert_element_type x2 -> x0, local copies, waits for them, and re-layouts: 102 us -> none  [the longest x1 65.1 us: local_layer(): jnp.einsum('tec,td->ecd', onehot, normed.reshape(tok_count, model_dim), p...]
    all_to_all x2 -> x0, local copies, waits for them, and re-layouts: 84.8 us -> none  [the longest x1 43.7 us: local_layer(): back_rows = lax.all_to_all(done_rows, 'ep', 1, 0, tiled=True)]
  transfers between devices with their start and end apart: 5 -> 6, of which waited for: 5 -> 6; matrix products, arithmetic and copies ran while one was open for 9% -> 13% of each run, Pallas kernels for 0% -> 0%
where the time goes in v1:
time: 806 us; the launch traced here: 797 us
  waiting for transfers between devices  510 us (63%)
  Pallas kernels  118 us (15%)
  matrix products  81.4 us (10%)
  other arithmetic  40.4 us (5%)
  blocking collectives  25.8 us (3%)
  between operations  14.2 us (2%)
    reduce_scatter x1, waiting for transfers between devices, local_layer(): mixed = lax.psum_scatter(partial, 'ep', scatter_dimension=0, tiled=True)  204 us
    pallas_call x1, Pallas kernels, moe_partial(): pl.pallas_call(functools.partial(moe_kernel, (total, cap_all, sub)), out_...  118 us
    all_gather x1, waiting for transfers between devices, local_layer(): full_key = lax.all_gather(w_key, 'ep', axis=0, tiled=True)  86.1 us
    all_gather x1, waiting for transfers between devices, local_layer(): full_query = lax.all_gather(w_query, 'ep', axis=0, tiled=True)  71.9 us
    all_gather x1, waiting for transfers between devices, local_layer(): full_out = lax.all_gather(w_out, 'ep', axis=0, tiled=True)  65.1 us
    all_gather x1, waiting for transfers between devices, local_layer(): full_value = lax.all_gather(w_value, 'ep', axis=0, tiled=True)  49.1 us
    all_gather x1, waiting for transfers between devices, local_layer(): lax.all_gather(normed.reshape(tok_count, model_dim // LANES, LANES), 'ep'...  30.8 us
    dot_general x1, matrix products, attention_layer(): jnp.einsum('bhqs,bshk->bqhk', attn_weights, values, preferred_element_typ...  20.7 us
  transfers between devices with their start and end apart: 6, of which 6 were waited for; matrix products, arithmetic and copies ran while one was open for 13% of the time, Pallas kernels for 0%

profile of v1, /device:TPU:0, one launch (start us, length us, event | category | flops | bytes accessed | tf_op | source)
XLA Modules:
  0.0 797.2 jit_solution(8556894042445730865)
XLA Ops:
  6.5 0.7 all-gather.11.cloned.1.call-update
  7.3 0.0 all-gather.9.cloned.1.call-start
  7.3 0.7 all-gather.9.cloned.1.call-update
  8.0 0.0 all-gather.7.cloned.1.call-start
  8.1 0.7 all-gather.7.cloned.1.call-update
  8.7 0.0 all-gather.13.cloned.1.call-start
  8.8 0.5 all-gather.13.cloned.1.call-update
  9.3 0.0 all-gather.15.cloned.1.call-start
  9.4 0.1 iota_compare_fusion.14
  9.5 0.5 fusion.17
  10.0 86.1 %all-gather.11.cloned.1.call-done = bf16[2048,16,256]{2,1,0:T(8,128)(2,1)} async-done(((bf16[256,16,256]{2,1,0:T(8,128)(2,1)}), bf16[2048,16,256]{2,1,0:T(8,128)(2,1)}) %all-gather.11.cloned.1.call-update) | async-done | bytes 16777232 | tf_op jit(solution)/shard_map/all_gather | solution.py:193
  96.1 14.0 %fusion.1 = bf16[512,16,256]{2,0,1:T(8,128)(2,1)} fusion(bf16[2048,16,256]{2,1,0:T(8,128)(2,1)} %all-gather.11.cloned.1.call-done, bf16[1,512,2048]{2,1,0:T(8,128)(2,1)S(1)} %copy-done.2, f32[512]{0:T(512)S(1)} %add_rsqrt_fusion.1), kind=kOutput, calls=%fused_computation.6 | convolution fusion | flops 8593080320 | bytes 23070720 | tf_op jit(solution)/shard_map/bsd,dhk->bshk/dot_general | solution.py:27
  110.1 71.9 %all-gather.9.cloned.1.call-done = bf16[2048,16,256]{2,1,0:T(8,128)(2,1)} async-done(((bf16[256,16,256]{2,1,0:T(8,128)(2,1)}), bf16[2048,16,256]{2,1,0:T(8,128)(2,1)}) %all-gather.9.cloned.1.call-update) | async-done | bytes 16777232 | tf_op jit(solution)/shard_map/all_gather | solution.py:192
  182.0 18.7 %fusion.22 = f32[16,512,512]{1,2,0:T(8,128)} fusion(bf16[512,16,256]{2,0,1:T(8,128)(2,1)} %fusion.1, bf16[2048,16,256]{2,1,0:T(8,128)(2,1)} %all-gather.9.cloned.1.call-done, bf16[1,512,2048]{2,1,0:T(8,128)(2,1)S(1)} %copy-done.2, f32[512]{0:T(512)S(1)} %add_rsqrt_fusion.1), kind=kOutput, calls=%fused_computation.40 | convolution fusion | flops 10742661120 | bytes 39847936 | tf_op jit(solution)/shard_map/bqhk,bshk->bhqs/dot_general | solution.py:29
  200.7 18.1 %fusion.56 = (f32[16,512]{1,0:T(8,128)S(1)}, f32[16,512,512]{1,2,0:T(8,128)}) fusion(f32[16,512,512]{1,2,0:T(8,128)} %fusion.22, pred[512,512]{0,1:T(8,128)(4,1)S(1)} %iota_compare_fusion.14), kind=kOutput, calls=%fused_computation.93 | output fusion | flops 25166336 | bytes 33849344 | tf_op jit(solution)/shard_map/sub | solution.py:31
  218.8 49.1 %all-gather.7.cloned.1.call-done = bf16[2048,16,256]{2,1,0:T(8,128)(2,1)} async-done(((bf16[256,16,256]{2,1,0:T(8,128)(2,1)}), bf16[2048,16,256]{2,1,0:T(8,128)(2,1)}) %all-gather.7.cloned.1.call-update) | async-done | bytes 16777232 | tf_op jit(solution)/shard_map/all_gather | solution.py:194
  267.9 20.7 %fusion.26 = bf16[16,256,512]{2,1,0:T(8,128)(2,1)} fusion(f32[16,512,512]{1,2,0:T(8,128)} %get-tuple-element.30, f32[16,512]{1,0:T(8,128)S(1)} %get-tuple-element.29, bf16[2048,16,256]{2,1,0:T(8,128)(2,1)} %all-gather.7.cloned.1.call-done, bf16[1,512,2048]{2,1,0:T(8,128)(2,1)S(1)} %copy-done.2, f32[512]{0:T(512)S(1)} %add_rsqrt_fusion.1), kind=kOutput, calls=%fused_computation.44 | convolution fusion | flops 10753146880 | bytes 39880704 | tf_op jit(solution)/shard_map/bhqs,bshk->bqhk/dot_general | solution.py:32
  288.7 65.1 %all-gather.13.cloned.1.call-done = bf16[4096,2048]{1,0:T(8,128)(2,1)} async-done(((bf16[512,2048]{1,0:T(8,128)(2,1)}), bf16[4096,2048]{1,0:T(8,128)(2,1)}) %all-gather.13.cloned.1.call-update) | async-done | bytes 16777232 | tf_op jit(solution)/shard_map/all_gather | solution.py:195
  353.7 14.2 %fusion.14 = (f32[512]{0:T(512)S(1)}, bf16[1,512,2048]{2,1,0:T(8,128)(2,1)S(1)}) fusion(bf16[512,4096]{0,1:T(8,128)(2,1)} %bitcast.101, bf16[4096,2048]{1,0:T(8,128)(2,1)} %all-gather.13.cloned.1.call-done, bf16[1,512,2048]{2,1,0:T(8,128)(2,1)} %param.10), kind=kOutput, calls=%fused_computation.32 | convolution fusion | flops 8596226048 | bytes 25167872 | tf_op jit(solution)/shard_map/crd,de->cre/dot_general | solution.py:33
  367.9 0.5 convert_bitcast_fusion
  368.4 0.9 copy.34
  369.4 0.0 copy-start.3
  369.4 2.8 fusion.21
  372.2 0.0 all-gather.15.cloned.1.call-update
  372.2 0.0 reduce-scatter.2.cloned.1.call-start
  372.3 12.5 %all-gather = s32[1,4096,10]{1,0,2:T(1,128)S(1)} all-gather(s32[1,512,10]{1,0,2:T(1,128)S(1)} %copy-done.3), channel_id=2, replica_groups=mesh['dp'=1,'ep'=8] {'ep'}, dimensions={1}, use_global_device_ids=true | all-gather | bytes 184320 | tf_op jit(solution)/shard_map/all_gather | solution.py:190
  384.8 0.4 subtract_reduce_fusion
  385.2 0.2 copy.33
  385.4 0.1 copy.29
  385.5 0.1 add_add_fusion
  385.6 5.8 convert_reduce_fusion
  391.5 0.1 lt.37
  391.6 2.0 fusion.32
  393.6 2.8 select_reduce_fusion
  396.5 0.1 add_select_fusion
  396.6 4.3 select_reduce_fusion.1
  400.9 0.1 sub.42
  401.0 0.6 compare_select_fusion.codes
  401.7 11.8 %select_reduce_fusion.3 = (f32[512]{0:T(512)S(1)}, f32[512]{0:T(512)S(1)}, f32[512]{0:T(512)S(1)}, f32[512]{0:T(512)S(1)}, f32[512]{0:T(512)S(1)}, /*index=5*/f3...) fusion(s32[512]{0:T(512)S(1)} %bitcast.100, s32[512]{0:T(512)S(1)} %bitcast.92, ...), kind=kOutput, calls=%fused_computation.50 | convolution fusion | flops 6452407296 | bytes 6334464 | tf_op jit(solution)/shard_map/dot_general | solution.py:39
  413.5 0.1 stack.43
  413.6 13.3 %all_gather.26 = f32[10,4096]{1,0:T(8,128)S(1)} all-gather(f32[10,512]{1,0:T(8,128)S(1)} %divide_bitcast_fusion), channel_id=1, replica_groups=mesh['dp'=1,'ep'=8] {'ep'}, dimensions={1}, use_global_device_ids=true | all-gather | bytes 184320 | tf_op jit(solution)/shard_map/all_gather | solution.py:199
  426.9 0.7 reshape.211.gates
  427.6 30.8 %all-gather.15.cloned.1.call-done.u_hbm = bf16[4096,16,128]{2,1,0:T(8,128)(2,1)} async-done(((bf16[512,16,128]{2,1,0:T(8,128)(2,1)}), bf16[4096,16,128]{2,1,0:T(8,128)(2,1)}) %all-gather.15.cloned.1.call-update) | async-done | bytes 16777232 | tf_op jit(solution)/shard_map/all_gather | solution.py:198
  458.4 118.5 %moe_partial.1 = f32[4096,16,128]{2,1,0:T(8,128)} custom-call(s32[10240]{0:T(1024)} %compare_select_fusion.codes, s32[64]{0:T(128)} %get-tuple-element.15.counts, f32[40960]{0:T(1024)} %reshape.211.gates, bf16[4096,16,128]{2,1,0:T(8,128)(2,1)} %all-gather.15.cloned.1.call-done.u_hbm, bf16[64,2048,128]{2,1,0:T(8,128)(2,1)} %w1_ref.1, ...), custom_call_target="tpu_custom_call" | custom-call | flops 9663676416 | bytes 150000000 | tf_op jit(solution)/shard_map/moe_partial/pallas_call | solution.py:151
  576.9 0.0 reduce-scatter.2.cloned.1.call-update
  576.9 203.9 %reduce-scatter.2.cloned.1.call-done = f32[512,16,128]{2,1,0:T(8,128)} async-done(((f32[4096,16,128]{2,1,0:T(8,128)}), f32[512,16,128]{2,1,0:T(8,128)}) %reduce-scatter.2.cloned.1.call-update) | async-done | bytes 4194320 | tf_op jit(solution)/shard_map/reduce_scatter | solution.py:201
  780.8 4.9 reshape.212
  785.7 4.2 fusion.20
  (28 shorter events, 0.2 us)
Async XLA Ops:
  6.5 2.9 copy-start.2
  6.5 89.6 %all-gather.11.cloned.1.call-start = ((), (), s32[]{:S(2)}) async-start(), calls=%async_computation.3 | async-start | bytes 18874368 | tf_op jit(solution)/shard_map/all_gather | solution.py:193
  7.3 174.8 %all-gather.9.cloned.1.call-start = ((), (), s32[]{:S(2)}) async-start(), calls=%async_computation.2 | async-start | bytes 18874368 | tf_op jit(solution)/shard_map/all_gather | solution.py:192
  8.0 259.9 %all-gather.7.cloned.1.call-start = ((), (), s32[]{:S(2)}) async-start(), calls=%async_computation.1 | async-start | bytes 18874368 | tf_op jit(solution)/shard_map/all_gather | solution.py:194
  8.7 345.0 %all-gather.13.cloned.1.call-start = ((), (), s32[]{:S(2)}) async-start(), calls=%async_computation.4 | async-start | bytes 18874368 | tf_op jit(solution)/shard_map/all_gather | solution.py:195
  9.3 449.1 %all-gather.15.cloned.1.call-start = ((), (), s32[]{:S(2)}) async-start(), calls=%async_computation.5 | async-start | bytes 18874368 | tf_op jit(solution)/shard_map/all_gather | solution.py:198
  367.9 33.8 %copy-start = (bf16[1,512,2048]{2,1,0:T(8,128)(2,1)}, bf16[1,512,2048]{2,1,0:T(8,128)(2,1)S(1)}, u32[]{:S(2)}) copy-start(bf16[1,512,2048]{2,1,0:T(8,128)(2,1)S(1)} %get-tuple-element.32) | copy-start | bytes 6291460
  369.4 2.9 copy-start.3
  372.2 408.6 %reduce-scatter.2.cloned.1.call-start = ((), (), s32[]{:S(2)}) async-start(), calls=%async_computation.6 | async-start | bytes 37748736 | tf_op jit(solution)/shard_map/reduce_scatter | solution.py:201
  576.9 208.8 %copy-start.1 = (bf16[1,512,2048]{2,1,0:T(8,128)(2,1)S(1)}, bf16[1,512,2048]{2,1,0:T(8,128)(2,1)}, u32[]{:S(2)}) copy-start(bf16[1,512,2048]{2,1,0:T(8,128)(2,1)} %copy-done) | copy-start | bytes 6291460
Sparse Core Ops, SparseCore 0:
  9.2 86.8 all-gather.10
  97.9 84.0 all-gather.8
  183.8 84.0 all-gather.6
  269.6 84.0 all-gather.12
  372.3 86.0 all-gather.14
  577.1 203.7 reduce-scatter.1
